TPU v7x, 32 devices: a whole 2x2x4 slice. The times are simulated.
32 devices in a mesh: band: 8 (over z, y), grid: 4 (over x, core).
Axes of the slice: x: 2, y: 2, z: 4, core: 2. Of those that a mesh axis runs over, the one named last changes fastest.
Arguments:
- orbitals: bfloat16 [8, 128, 128, 128], P('band', 'grid'), may hold values from -3 to 3
- trial_vectors: bfloat16 [2, 8, 128, 128, 128], P(None, 'band', 'grid'), may hold values from -6 to 6
- alda_kernel: float32 [128, 128, 128], P('grid'), may hold values from -2 to -0.5
- local_potential: float32 [128, 128, 128], P('grid'), may hold values from -2 to 1
- band_energies: float32 [8], P('band'), may hold values from -1.5 to -0.2
Outputs:
- sigma_real: float32 [2, 8, 128, 128, 128], P(None, 'band', 'grid')
- sigma_imag: float32 [2, 8, 128, 128, 128], P(None, 'band', 'grid')
All inputs are finite; a program needn't handle non-finite values.
Results may differ from a plain program's by a relative error of at most 0.0003.
Values sent between devices are 32-bit elements; how exact they have to be, the bound alone decides.
A program may use at most 64 MiB of HBM per device.

v0:
```python
import math

import jax
import jax.numpy as jnp
from jax import lax
from jax.sharding import PartitionSpec as P

box_length = 30.0
highest = lax.Precision.HIGHEST


def tables(length):
    positions = jnp.arange(length, dtype=jnp.int32)
    wrapped = positions[:, None] * positions[None, :] % length
    angles = wrapped.astype(jnp.float32) * (2.0 * math.pi / length)
    return (jnp.cos(angles), jnp.sin(angles))


def contract(pattern, left_operand, right_operand):
    return jnp.einsum(pattern, left_operand, right_operand, precision=highest)


def rotate(pattern, real_part, imag_part, cosine_table, sine_table, orient):
    new_real = contract(pattern, real_part, cosine_table) - orient * contract(
        pattern, imag_part, sine_table
    )
    new_imag = contract(pattern, imag_part, cosine_table) + orient * contract(
        pattern, real_part, sine_table
    )
    return (new_real, new_imag)


def rotate_real(pattern, real_part, cosine_table, sine_table, orient):
    return (
        contract(pattern, real_part, cosine_table),
        orient * contract(pattern, real_part, sine_table),
    )


def frequency(length, offset, extent):
    positions = offset + jnp.arange(extent, dtype=jnp.int32)
    signed = jnp.where(2 * positions < length, positions, positions - length)
    return signed.astype(jnp.float32)


def coulomb(first_freq, second_freq, third_freq):
    squared = (
        first_freq[:, None, None] ** 2
        + second_freq[None, :, None] ** 2
        + third_freq[None, None, :] ** 2
    )
    scaled = box_length**2 / math.pi / jnp.maximum(squared, 1.0)
    return jnp.where(squared > 0, scaled, 0.0)


def potential_split(density_share, cosine_table, sine_table, length):
    real_part, imag_part = rotate_real(
        "kxyz,zg->kxgy", density_share, cosine_table, sine_table, -1.0
    )
    arrived = lax.all_to_all(
        jnp.stack((real_part, imag_part)), "band", split_axis=3, concat_axis=4, tiled=True
    )
    real_part, imag_part = rotate(
        "kxzy,yg->kgzx", arrived[0], arrived[1], cosine_table, sine_table, -1.0
    )
    arrived = lax.all_to_all(
        jnp.stack((real_part, imag_part)), "grid", split_axis=2, concat_axis=4, tiled=True
    )
    real_part, imag_part = rotate(
        "kyzx,xg->kyzg", arrived[0], arrived[1], cosine_table, sine_table, -1.0
    )
    rows_here = real_part.shape[1]
    planes_here = real_part.shape[2]
    kernel = coulomb(
        frequency(length, lax.axis_index("grid") * rows_here, rows_here),
        frequency(length, lax.axis_index("band") * planes_here, planes_here),
        frequency(length, 0, length),
    )
    real_part = real_part * kernel[None]
    imag_part = imag_part * kernel[None]
    real_part, imag_part = rotate(
        "kyzg,gx->kyzx", real_part, imag_part, cosine_table, sine_table, 1.0
    )
    arrived = lax.all_to_all(
        jnp.stack((real_part, imag_part)), "grid", split_axis=4, concat_axis=2, tiled=True
    )
    real_part, imag_part = rotate(
        "kgzx,gy->kxzy", arrived[0], arrived[1], cosine_table, sine_table, 1.0
    )
    arrived = lax.all_to_all(
        jnp.stack((real_part, imag_part)), "band", split_axis=4, concat_axis=3, tiled=True
    )
    restored = contract("kxgy,gz->kxyz", arrived[0], cosine_table) - contract(
        "kxgy,gz->kxyz", arrived[1], sine_table
    )
    return restored / float(length**3)


def per_device(orbitals, trial_vectors, alda_kernel, local_potential, band_energies):
    length = orbitals.shape[2]
    cosine_table, sine_table = tables(length)
    orbital_wide = orbitals.astype(jnp.float32)
    trial_wide = trial_vectors.astype(jnp.float32)
    partial_value = 2.0 * jnp.sum(trial_wide * orbital_wide[None], axis=1)
    density_share = lax.psum_scatter(partial_value, "band", scatter_dimension=2, tiled=True)
    row_count = density_share.shape[2]
    kernel_rows = lax.dynamic_slice_in_dim(
        alda_kernel, lax.axis_index("band") * row_count, row_count, 1
    )
    hartree = potential_split(density_share, cosine_table, sine_table, length)
    potential = lax.all_gather(
        hartree + kernel_rows[None] * density_share, "band", axis=2, tiled=True
    )
    weight = local_potential[None] - band_energies[:, None, None, None]
    fields = potential[:, None] * orbital_wide[None] + weight[None] * trial_wide
    trial_count = trial_vectors.shape[0]
    norm_factor = float(length) ** (-1.5)
    pieces = []
    for trial_index in range(trial_count):
        real_part, imag_part = rotate_real(
            "mxyz,zg->mxyg", fields[trial_index], cosine_table, sine_table, -1.0
        )
        real_part, imag_part = rotate(
            "mxyz,yg->mgzx", real_part, imag_part, cosine_table, sine_table, -1.0
        )
        received = lax.all_to_all(
            jnp.stack((real_part, imag_part)), "grid", split_axis=2, concat_axis=4, tiled=True
        )
        finish_real_part, finish_imag_part = rotate(
            "myzx,xg->myzg", received[0], received[1], cosine_table, sine_table, -1.0
        )
        pieces.append(jnp.stack((finish_real_part * norm_factor, finish_imag_part * norm_factor)))
    results = jnp.stack(pieces, axis=1)
    return (results[0], results[1])


def solution(mesh):
    placed = (
        P("band", "grid", None, None),
        P(None, "band", "grid", None, None),
        P("grid", None, None),
        P("grid", None, None),
        P("band"),
    )
    return jax.shard_map(
        per_device,
        mesh=mesh,
        in_specs=placed,
        out_specs=(P(None, "band", "grid", None, None), P(None, "band", "grid", None, None)),
        check_vma=False,
    )
```

profile of v0, /device:TPU:0, one launch (start us, length us, event | category | flops | bytes accessed | tf_op | source)
XLA Modules:
  0.0 582.9 jit_solution(3529673383581125716)
XLA Ops:
  13.0 91.5 %reduce-scatter.2.cloned.1.call-done = f32[2,32,16,128]{3,2,1,0:T(8,128)} async-done(((f32[2,32,128,128]{3,2,1,0:T(8,128)}), f32[2,32,16,128]{3,2,1,0:T(8,128)}) %reduce-scatter.2.cloned.1.call-update) | async-done | bytes 524304 | tf_op jit(solution)/shard_map/reduce_scatter | solution.py:105
  112.8 4.8 reshape.245
  117.6 4.6 all-to-all-start
  122.2 25.6 %all-to-all-done = f32[8,1,32768]{2,1,0:T(1,128)S(1)} async-done(((f32[8,1,32768]{2,1,0:T(1,128)}), f32[8,1,32768]{2,1,0:T(1,128)S(1)}, u32[]{:S(2)}, u32[]{:S(2)}) %all-to-all-start) | async-done | bytes 1048608 | tf_op jit(solution)/shard_map/all_to_all | solution.py:60
  167.6 14.0 %fusion.27 = f32[1,2,128,16,32]{2,4,3,1,0:T(8,128)S(1)} fusion(f32[128,2,32,16]{0,2,3,1:T(8,128)S(1)} %convolution_multiply_fusion.1, f32[2,32,16,128]{1,3,2,0:T(8,128)S(1)} %bitcast.275), kind=kOutput, calls=%fused_computation.44 | convolution fusion | flops 201687040 | bytes 1572864 | tf_op jit(solution)/shard_map/kxzy,yg->kgzx/dot_general | solution.py:20
  189.5 4.8 reshape.247
  198.9 14.2 %all-to-all-done.1 = f32[4,1,65536]{2,1,0:T(1,128)} async-done(((f32[4,1,65536]{2,1,0:T(1,128)}), f32[4,1,65536]{2,1,0:T(1,128)}, u32[]{:S(2)}, u32[]{:S(2)}) %all-to-all-start.1) | async-done | bytes 1048608 | tf_op jit(solution)/shard_map/all_to_all | solution.py:66
  213.1 4.6 reduce.1
  221.2 4.9 copy.248
  248.7 17.7 %all_to_all.90 = f32[4,1,65536]{2,1,0:T(1,128)} all-to-all(f32[4,1,65536]{2,1,0:T(1,128)S(1)} %reshape.249), channel_id=1, replica_groups=mesh['band'=8,'grid'=4] {'grid'}, dimensions={0} | all-to-all | bytes 2097152 | tf_op jit(solution)/shard_map/all_to_all | solution.py:84
  266.4 4.6 reduce.2
  274.5 4.9 copy.247
  295.3 4.8 reshape.251
  304.3 25.1 %all-to-all-done.3 = f32[8,1,32768]{2,1,0:T(1,128)S(1)} async-done(((f32[8,1,32768]{2,1,0:T(1,128)}), f32[8,1,32768]{2,1,0:T(1,128)S(1)}, u32[]{:S(2)}, u32[]{:S(2)}) %all-to-all-start.3) | async-done | bytes 1048608 | tf_op jit(solution)/shard_map/all_to_all | solution.py:90
  335.9 4.6 copy.179
  354.4 69.1 %all-gather.2.cloned.1.call-done = f32[2,32,128,128]{3,2,1,0:T(8,128)} async-done(((f32[2,32,16,128]{3,2,1,0:T(8,128)}), f32[2,32,128,128]{3,2,1,0:T(8,128)}) %all-gather.2.cloned.1.call-update) | async-done | bytes 4194320 | tf_op jit(solution)/shard_map/all_gather | solution.py:111
  423.5 4.7 fusion.2
  442.3 4.4 copy.188
  446.7 4.8 all-to-all-start.4
  471.6 28.2 %all-to-all-done.4 = f32[2,1,128,128,32]{3,4,1,0,2:T(8,128)} async-done(((f32[2,1,128,128,32]{3,4,1,0,2:T(8,128)}), f32[2,1,128,128,32]{3,4,1,0,2:T(8,128)}, u32[]{:S(2)}, u32[]{:S(2)}) %all-to-all-start.4) | async-done | bytes 4194336 | tf_op jit(solution)/shard_map/all_to_all | solution.py:126
  499.8 4.9 all-to-all-start.5
  511.9 5.0 multiply_bitcast_fusion.3
  521.0 4.9 multiply_bitcast_fusion.2
  525.9 26.9 %all-to-all-done.5 = f32[2,1,128,128,32]{3,4,1,0,2:T(8,128)} async-done(((f32[2,1,128,128,32]{3,4,1,0,2:T(8,128)}), f32[2,1,128,128,32]{3,4,1,0,2:T(8,128)}, u32[]{:S(2)}, u32[]{:S(2)}) %all-to-all-start.5) | async-done | bytes 4194336 | tf_op jit(solution)/shard_map/all_to_all | solution.py:126
  (122 shorter events, 183.3 us)
Async XLA Ops:
  7.2 297.1 %copy-start = (f32[32,128,128]{2,1,0:T(8,128)S(1)}, f32[32,128,128]{2,1,0:T(8,128)}, u32[]{:S(2)}) copy-start(f32[32,128,128]{2,1,0:T(8,128)} %param.7) | copy-start | bytes 6291460
  7.2 97.3 %reduce-scatter.2.cloned.1.call-start = ((), (), s32[]{:S(2)}) async-start(), calls=%async_computation.7 | async-start | bytes 4718592 | tf_op jit(solution)/shard_map/reduce_scatter | solution.py:105
  7.2 3.0 copy-start.6
  8.9 1.4 copy-start.4
  117.6 30.2 %all-to-all-start = ((f32[8,1,32768]{2,1,0:T(1,128)}), f32[8,1,32768]{2,1,0:T(1,128)S(1)}, u32[]{:S(2)}, u32[]{:S(2)}) async-start(f32[8,1,32768]{2,1,0:T(1,128)} %reshape.245), calls=%async_computation.1 | async-start | bytes 2097152 | tf_op jit(solution)/shard_map/all_to_all | solution.py:60
  147.9 1.0 copy-start.10
  194.4 18.7 %all-to-all-start.1 = ((f32[4,1,65536]{2,1,0:T(1,128)}), f32[4,1,65536]{2,1,0:T(1,128)}, u32[]{:S(2)}, u32[]{:S(2)}) async-start(f32[4,1,65536]{2,1,0:T(1,128)} %reshape.247), calls=%async_computation.2 | async-start | bytes 2097152 | tf_op jit(solution)/shard_map/all_to_all | solution.py:66
  289.0 1.7 copy-start.11
  300.2 29.2 %all-to-all-start.3 = ((f32[8,1,32768]{2,1,0:T(1,128)}), f32[8,1,32768]{2,1,0:T(1,128)S(1)}, u32[]{:S(2)}, u32[]{:S(2)}) async-start(f32[8,1,32768]{2,1,0:T(1,128)} %reshape.251), calls=%async_computation.4 | async-start | bytes 2097152 | tf_op jit(solution)/shard_map/all_to_all | solution.py:90
  303.8 119.7 %all-gather.2.cloned.1.call-start = ((), (), s32[]{:S(2)}) async-start(), calls=%async_computation.8 | async-start | bytes 4718592 | tf_op jit(solution)/shard_map/all_gather | solution.py:111
  346.0 1.7 copy-start.9
  351.1 72.4 %copy-start.5 = (f32[32,128,128]{2,1,0:T(8,128)S(1)}, f32[32,128,128]{2,1,0:T(8,128)}, u32[]{:S(2)}) copy-start(f32[32,128,128]{2,1,0:T(8,128)} %copy-done.4) | copy-start | bytes 6291460
  428.2 2.1 copy-start.2
  446.7 53.1 %all-to-all-start.4 = ((f32[2,1,128,128,32]{3,4,1,0,2:T(8,128)}), f32[2,1,128,128,32]{3,4,1,0,2:T(8,128)}, u32[]{:S(2)}, u32[]{:S(2)}) async-start(f32[2,1,128,128,32]{3,4,1,0,2:T(8,128)} %copy.188), calls=%async_computation.5 | async-start | bytes 8388608 | tf_op jit(solution)/shard_map/all_to_all | solution.py:126
  451.6 3.8 copy-start.3
  499.8 53.1 %all-to-all-start.5 = ((f32[2,1,128,128,32]{3,4,1,0,2:T(8,128)}), f32[2,1,128,128,32]{3,4,1,0,2:T(8,128)}, u32[]{:S(2)}, u32[]{:S(2)}) async-start(f32[2,1,128,128,32]{3,4,1,0,2:T(8,128)} %copy.201), calls=%async_computation.6 | async-start | bytes 8388608 | tf_op jit(solution)/shard_map/all_to_all | solution.py:126
  567.6 3.6 copy-start.7
  567.6 3.6 copy-start.8
  572.2 3.6 copy-start.1
Sparse Core Ops, SparseCore 0:
  13.1 91.3 reduce-scatter.1
  350.5 72.9 all-gather.1
where the time goes:
time: 588 us; the launch traced here: 583 us
  waiting for transfers between devices  281 us (48%)
  local copies, waits for them, and re-layouts  108 us (18%)
  matrix products  103 us (18%)
  other arithmetic  35.2 us (6%)
  starting transfers between devices  22.7 us (4%)
  blocking collectives  17.7 us (3%)
  between operations  15.6 us (3%)
    dot_general x36, matrix products, contract(): return jnp.einsum(pattern, left_operand, right_operand, precision=highest)  99 us
    reduce_scatter x1, waiting for transfers between devices, per_device(): lax.psum_scatter(partial_value, 'band', scatter_dimension=2, tiled=True)  91.5 us
    all_gather x1, waiting for transfers between devices, per_device(): lax.all_gather(hartree + kernel_rows[None] * density_share, 'band', axis=...  69.1 us
    all_to_all x2, waiting for transfers between devices, per_device(): lax.all_to_all(jnp.stack((real_part, imag_part)), 'grid', split_axis=2, c...  55.1 us
    unnamed x32, local copies, waits for them, and re-layouts  34.5 us
    all_to_all x1, waiting for transfers between devices, potential_split(): lax.all_to_all(jnp.stack((real_part, imag_part)), 'band', split_axis=3, c...  25.6 us
    all_to_all x1, waiting for transfers between devices, potential_split(): lax.all_to_all(jnp.stack((real_part, imag_part)), 'band', split_axis=4, c...  25.1 us
    all_to_all x1, blocking collectives, potential_split(): lax.all_to_all(jnp.stack((real_part, imag_part)), 'grid', split_axis=4, c...  17.7 us
  transfers between devices with their start and end apart: 7, of which 7 were waited for; matrix products, arithmetic and copies ran while one was open for 8% of the time, Pallas kernels for 0%

commit v1 on v0

--- a/solution.py
+++ b/solution.py
@@ -1,12 +1,18 @@
+import functools
 import math
 
 import jax
 import jax.numpy as jnp
+import numpy as np
 from jax import lax
+from jax.experimental import pallas as pl
+from jax.experimental.pallas import tpu as pltpu
 from jax.sharding import PartitionSpec as P
 
 box_length = 30.0
+f32, bf16 = jnp.float32, jnp.bfloat16
 highest = lax.Precision.HIGHEST
+vmem_grant = 56 * 1024 * 1024
 
 
 def tables(length):
@@ -43,7 +49,7 @@
     return signed.astype(jnp.float32)
 
 
-def coulomb(first_freq, second_freq, third_freq):
+def coulomb_block(first_freq, second_freq, third_freq):
     squared = (
         first_freq[:, None, None] ** 2
         + second_freq[None, :, None] ** 2
@@ -71,7 +77,7 @@
     )
     rows_here = real_part.shape[1]
     planes_here = real_part.shape[2]
-    kernel = coulomb(
+    kernel = coulomb_block(
         frequency(length, lax.axis_index("grid") * rows_here, rows_here),
         frequency(length, lax.axis_index("band") * planes_here, planes_here),
         frequency(length, 0, length),
@@ -96,42 +102,311 @@
     return restored / float(length**3)
 
 
-def per_device(orbitals, trial_vectors, alda_kernel, local_potential, band_energies):
+def halves(table):
+    table = np.asarray(table, np.float32)
+    high = table.astype(bf16)
+    low = (table - high.astype(np.float32)).astype(bf16)
+    return jnp.asarray(high), jnp.asarray(low)
+
+
+def waves(length, orient):
+    index = np.arange(length)
+    angles = (index[:, None] * index[None, :] % length) * (2.0 * np.pi / length)
+    return np.cos(angles), orient * np.sin(angles)
+
+
+def right_block(length, orient):
+    cosine, sine = waves(length, orient)
+    return np.block([[cosine, sine], [-sine, cosine]])
+
+
+def split(value):
+    high = value.astype(bf16)
+    return high, (value - high.astype(f32)).astype(bf16)
+
+
+def mm(left, right):
+    return jnp.dot(left, right, preferred_element_type=f32)
+
+
+def times(value, high, low):
+    value_high, value_low = split(value)
+    return mm(value_high, high) + (mm(value_low, high) + mm(value_high, low))
+
+
+def table_times(high, low, value):
+    value_high, value_low = split(value)
+    return mm(high, value_high) + (mm(high, value_low) + mm(low, value_high))
+
+
+def plane_forward(length, share, d_ref, zh, zl, yh, yl, out_ref):
+    for x in range(share):
+        pair = jnp.concatenate([d_ref[x, 0], d_ref[x, 1]], axis=1)
+        spec = times(pair, zh[...], zl[...])
+        spec = jnp.concatenate([spec[:, :length], spec[:, length:]], axis=0)
+        spec = table_times(yh[...], yl[...], spec)
+        for part in range(2):
+            out_ref[pl.ds(part * share + x, length, stride=2 * share), :] = spec[
+                part * length : (part + 1) * length
+            ]
+
+
+def column_filter(length, bs, v_ref, k_ref, fh, fl, ih, il, out_ref):
+    if bs == 1:
+        values = v_ref[...]
+    else:
+        values = jnp.concatenate(
+            [v_ref[:, b].reshape(2 * length, length) for b in range(bs)], axis=1
+        )
+    spec = table_times(fh[...], fl[...], values)
+    kern = k_ref[...]
+    spec = jnp.concatenate([spec[:length] * kern, spec[length:] * kern], axis=0)
+    back = table_times(ih[...], il[...], spec)
+    if bs == 1:
+        out_ref[...] = back
+    else:
+        for b in range(bs):
+            out_ref[:, b] = back[:, b * length : (b + 1) * length].reshape(
+                out_ref.shape[0], out_ref.shape[2], length
+            )
+
+
+def plane_backward(length, share, v_ref, d_ref, a_ref, yh, yl, zh, zl, out_ref):
+    for x in range(share):
+        spec = jnp.concatenate(
+            [
+                v_ref[pl.ds(part * share + x, length, stride=2 * share), :]
+                for part in range(2)
+            ],
+            axis=0,
+        )
+        spec = table_times(yh[...], yl[...], spec)
+        spec = jnp.concatenate([spec[:length], spec[length:]], axis=1)
+        spec = times(spec, zh[...], zl[...])
+        for k in range(2):
+            out_ref[x, k] = (
+                spec[:, k * length : (k + 1) * length] + a_ref[x] * d_ref[x, k]
+            )
+
+
+def field_forward(length, rows, groups, e_ref, p_ref, o_ref, t_ref, l_ref, zh, zl, yh, yl, out_ref):
+    width = length // groups
+    energy = e_ref[0]
+    fields = p_ref[...] * o_ref[...].astype(f32) + (l_ref[...] - energy) * t_ref[
+        ...
+    ].astype(f32)
+    spec = times(fields.reshape(rows * length, length), zh[...], zl[...])
+    for x in range(0, rows, 2):
+        pair = jnp.concatenate(
+            [
+                jnp.concatenate(
+                    [
+                        spec[i * length : (i + 1) * length, :length],
+                        spec[i * length : (i + 1) * length, length:],
+                    ],
+                    axis=0,
+                )
+                for i in (x, x + 1)
+            ],
+            axis=1,
+        )
+        pair = table_times(yh[...], yl[...], pair)
+        for i in range(2):
+            for part in range(2):
+                for g in range(groups):
+                    start = part * length + g * width
+                    out_ref[g, 0, part, pl.ds(x + i, width, stride=rows), :] = pair[
+                        start : start + width, i * length : (i + 1) * length
+                    ]
+
+
+def field_finish(length, rows, count, v_ref, wh, wl, *refs):
+    real_ref, imag_ref = refs[-2:]
+    for b in range(count):
+        value = v_ref[:, :, :, b * rows : (b + 1) * rows, :].reshape(2 * length, length)
+        done = times(value.T, wh[...], wl[...])
+        real_ref[b] = done[:, :length]
+        imag_ref[b] = done[:, length:]
+
+
+def whole_spec(count):
+    return [pl.BlockSpec(memory_space=pltpu.VMEM)] * count
+
+
+def cost(flops, size):
+    return pl.CostEstimate(flops=flops, bytes_accessed=size, transcendentals=0)
+
+
+def coulomb(length, second, cells):
+    def signed(position):
+        return jnp.where(2 * position < length, position, position - length).astype(f32)
+
+    along = signed(jnp.arange(length, dtype=jnp.int32))
+    squared = (
+        along[:, None, None] ** 2
+        + signed(second)[None, :, None] ** 2
+        + along[None, None, :] ** 2
+    )
+    scaled = (box_length**2 / math.pi / cells) / jnp.maximum(squared, 1.0)
+    return jnp.where(squared > 0, scaled, 0.0)
+
+
+def plane_potential(bands, groups, orbital, trial, alda_kernel):
+    length, x_here = orbital.shape[1], orbital.shape[0]
+    share = x_here // bands
+    params = pltpu.CompilerParams(vmem_limit_bytes=vmem_grant)
+    forward = right_block(length, -1.0)
+    backward = right_block(length, 1.0)
+    devices = bands * groups
+    bs = length // devices
+    unit = 2 * length**3
+
+    partial_value = 2.0 * (trial.astype(f32) * orbital.astype(f32)[None])
+    partial_value = partial_value.reshape(2, bands, share * length // 16, 16, length)
+    partial_value = partial_value.swapaxes(1, 2).reshape(2, -1, bands * 16, length)
+    density = lax.psum_scatter(partial_value, "band", scatter_dimension=2, tiled=True)
+    density = density.reshape(2, share, length, length).transpose(1, 0, 2, 3)
+    alda_rows = lax.dynamic_slice_in_dim(
+        alda_kernel, lax.axis_index("band") * share, share, 0
+    )
+    here = lax.axis_index("band") * groups + lax.axis_index("grid")
+    kern = coulomb(
+        length, here * bs + jnp.arange(bs, dtype=jnp.int32), float(length**3)
+    ).reshape(length, bs * length)
+
+    index = np.arange(devices * 2 * share).reshape(bands, groups, 2, share)
+    band_i, grid_i, part_i, row_i = np.unravel_index(index, index.shape)
+    order = (part_i * length + grid_i * x_here + band_i * share + row_i).reshape(-1)
+    fwd_right, bwd_right = halves(forward), halves(backward)
+    fwd_left, bwd_left = halves(forward.T), halves(backward.T)
+    column_fwd = halves(forward.T[:, order])
+    column_bwd = halves(backward.T[order, :])
+
+    flat = (length * 2 * share, length)
+    sent = pl.pallas_call(
+        functools.partial(plane_forward, length, share),
+        out_shape=jax.ShapeDtypeStruct(flat, f32),
+        in_specs=whole_spec(5),
+        out_specs=whole_spec(1)[0],
+        compiler_params=params,
+        cost_estimate=cost(24 * share * unit, 8 * share * length**2 * 4),
+    )(density, *fwd_right, *fwd_left)
+
+    both = ("band", "grid")
+    block = (devices, bs * 2 * share, length)
+    came = lax.all_to_all(sent.reshape(block), both, 0, 0, tiled=True)
+    shape = flat if bs == 1 else (devices, bs, 2 * share, length)
+    sent = pl.pallas_call(
+        functools.partial(column_filter, length, bs),
+        out_shape=jax.ShapeDtypeStruct(shape, f32),
+        in_specs=whole_spec(6),
+        out_specs=whole_spec(1)[0],
+        compiler_params=params,
+        cost_estimate=cost(24 * bs * unit, 8 * share * length**2 * 4),
+    )(came.reshape(shape), kern, *column_fwd, *column_bwd)
+    came = lax.all_to_all(sent.reshape(block), both, 0, 0, tiled=True)
+    potential_rows = pl.pallas_call(
+        functools.partial(plane_backward, length, share),
+        out_shape=jax.ShapeDtypeStruct(density.shape, f32),
+        in_specs=whole_spec(7),
+        out_specs=whole_spec(1)[0],
+        compiler_params=params,
+        cost_estimate=cost(24 * share * unit, 8 * share * length**2 * 4),
+    )(came.reshape(flat), density, alda_rows, *bwd_left, *bwd_right)
+    return lax.all_gather(potential_rows, "band", axis=0, tiled=True)
+
+
+def pencil_potential(orbital, trial, alda_kernel):
+    length = orbital.shape[1]
+    cosine_table, sine_table = tables(length)
+    partial_value = 2.0 * (trial.astype(f32) * orbital.astype(f32)[None])
+    density = lax.psum_scatter(partial_value, "band", scatter_dimension=2, tiled=True)
+    count = density.shape[2]
+    alda_rows = lax.dynamic_slice_in_dim(
+        alda_kernel, lax.axis_index("band") * count, count, 1
+    )
+    hartree = potential_split(density, cosine_table, sine_table, length)
+    potential = lax.all_gather(
+        hartree + alda_rows[None] * density, "band", axis=2, tiled=True
+    )
+    return potential.transpose(1, 0, 2, 3)
+
+
+def per_device(bands, groups, orbitals, trial_vectors, alda_kernel, local_potential, band_energies):
     length = orbitals.shape[2]
-    cosine_table, sine_table = tables(length)
-    orbital_wide = orbitals.astype(jnp.float32)
-    trial_wide = trial_vectors.astype(jnp.float32)
-    partial_value = 2.0 * jnp.sum(trial_wide * orbital_wide[None], axis=1)
-    density_share = lax.psum_scatter(partial_value, "band", scatter_dimension=2, tiled=True)
-    row_count = density_share.shape[2]
-    kernel_rows = lax.dynamic_slice_in_dim(
-        alda_kernel, lax.axis_index("band") * row_count, row_count, 1
-    )
-    hartree = potential_split(density_share, cosine_table, sine_table, length)
-    potential = lax.all_gather(
-        hartree + kernel_rows[None] * density_share, "band", axis=2, tiled=True
-    )
-    weight = local_potential[None] - band_energies[:, None, None, None]
-    fields = potential[:, None] * orbital_wide[None] + weight[None] * trial_wide
-    trial_count = trial_vectors.shape[0]
-    norm_factor = float(length) ** (-1.5)
-    pieces = []
-    for trial_index in range(trial_count):
-        real_part, imag_part = rotate_real(
-            "mxyz,zg->mxyg", fields[trial_index], cosine_table, sine_table, -1.0
+    x_here = orbitals.shape[1]
+    orbital, trial = orbitals[0], trial_vectors[:, 0]
+    params = pltpu.CompilerParams(vmem_limit_bytes=vmem_grant)
+    unit = 2 * length**3
+    forward = right_block(length, -1.0)
+    fwd_left = halves(forward.T)
+    if x_here % bands == 0 and length % (bands * groups) == 0 and trial.shape[0] == 2:
+        potential = plane_potential(bands, groups, orbital, trial, alda_kernel)
+    else:
+        potential = pencil_potential(orbital, trial, alda_kernel)
+
+    rows = 8
+    steps = x_here // rows
+    width = length // groups
+    z_table = halves(forward[:length])
+    index = np.arange(2 * length).reshape(groups, steps, 2, rows)
+    grid_i, step_i, part_i, row_i = np.unravel_index(index, index.shape)
+    order = (part_i * length + grid_i * x_here + step_i * rows + row_i).reshape(-1)
+    x_table = halves((forward * float(length) ** -1.5)[order])
+    trial_count = trial.shape[0]
+    table_spec = lambda a, b: pl.BlockSpec((a, b), lambda i: (0, 0))
+    cube = (rows, length, length)
+    squeezed = pl.Squeezed()
+    came = []
+    for k in range(trial_count):
+        sent = pl.pallas_call(
+            functools.partial(field_forward, length, rows, groups),
+            grid=(steps,),
+            out_shape=jax.ShapeDtypeStruct((groups, steps, 2, width * rows, length), f32),
+            in_specs=[
+                pl.BlockSpec(memory_space=pltpu.SMEM),
+                pl.BlockSpec((rows, squeezed, length, length), lambda i, k=k: (i, k, 0, 0)),
+                pl.BlockSpec(cube, lambda i: (i, 0, 0)),
+                pl.BlockSpec((squeezed, *cube), lambda i, k=k: (k, i, 0, 0)),
+                pl.BlockSpec(cube, lambda i: (i, 0, 0)),
+                table_spec(length, 2 * length),
+                table_spec(length, 2 * length),
+                table_spec(2 * length, 2 * length),
+                table_spec(2 * length, 2 * length),
+            ],
+            out_specs=pl.BlockSpec(
+                (groups, 1, 2, width * rows, length), lambda i: (0, i, 0, 0, 0)
+            ),
+            compiler_params=params,
+            cost_estimate=cost(18 * x_here * unit, 8 * x_here * length**2 * 4),
+        )(band_energies, potential, orbital, trial, local_potential, *z_table, *fwd_left)
+        came.append(lax.all_to_all(sent, "grid", 0, 0, tiled=True))
+
+    count = 8
+    full = jax.ShapeDtypeStruct((trial_count, 1, width, length, length), f32)
+    results = ()
+    for k in range(trial_count):
+        out_spec = pl.BlockSpec(
+            (squeezed, squeezed, count, length, length), lambda i, k=k: (k, 0, i, 0, 0)
         )
-        real_part, imag_part = rotate(
-            "mxyz,yg->mgzx", real_part, imag_part, cosine_table, sine_table, -1.0
-        )
-        received = lax.all_to_all(
-            jnp.stack((real_part, imag_part)), "grid", split_axis=2, concat_axis=4, tiled=True
-        )
-        finish_real_part, finish_imag_part = rotate(
-            "myzx,xg->myzg", received[0], received[1], cosine_table, sine_table, -1.0
-        )
-        pieces.append(jnp.stack((finish_real_part * norm_factor, finish_imag_part * norm_factor)))
-    results = jnp.stack(pieces, axis=1)
-    return (results[0], results[1])
+        results = pl.pallas_call(
+            functools.partial(field_finish, length, rows, count),
+            grid=(width // count,),
+            out_shape=(full, full),
+            in_specs=[
+                pl.BlockSpec(
+                    (groups, steps, 2, count * rows, length), lambda i: (0, 0, 0, i, 0)
+                ),
+                table_spec(2 * length, 2 * length),
+                table_spec(2 * length, 2 * length),
+            ]
+            + [pl.BlockSpec(memory_space=pl.ANY)] * len(results),
+            out_specs=(out_spec, out_spec),
+            input_output_aliases={3: 0, 4: 1} if results else {},
+            compiler_params=params,
+            cost_estimate=cost(12 * width * unit, 16 * x_here * length**2 * 4),
+        )(came[k], *x_table, *results)
+    return tuple(results)
 
 
 def solution(mesh):
@@ -142,10 +417,11 @@
         P("grid", None, None),
         P("band"),
     )
+    out = P(None, "band", "grid", None, None)
     return jax.shard_map(
-        per_device,
+        functools.partial(per_device, mesh.shape["band"], mesh.shape["grid"]),
         mesh=mesh,
         in_specs=placed,
-        out_specs=(P(None, "band", "grid", None, None), P(None, "band", "grid", None, None)),
+        out_specs=(out, out),
         check_vma=False,
     )

time: 588 us -> 356 us (0.61)
  matrix products: 103 us -> 0 us
  local copies, waits for them, and re-layouts: 108 us -> 7.5 us
  Pallas kernels: 0 us -> 40.4 us
  other arithmetic: 35.2 us -> 2.97 us
  blocking collectives: 17.7 us -> 0 us
  waiting for transfers between devices: 281 us -> 273 us
    dot_general x36 -> x0, matrix products: 99 us -> none  [contract(): return jnp.einsum(pattern, left_operand, right_operand, precision=highest)]
    pallas_call x0 -> x7, Pallas kernels: none -> 40.4 us  [the longest x2 18.6 us: per_device(): pl.pallas_call(functools.partial(field_forward, length, rows, groups), gr...]
    unnamed x32 -> x8, local copies, waits for them, and re-layouts: 34.5 us -> 2.07 us
    another operation x6 -> x0, local copies, waits for them, and re-layouts: 26.5 us -> none  [the longest x4 17.6 us: potential_split(): jnp.stack((real_part, imag_part))]
    all_to_all x7 -> x0, local copies, waits for them, and re-layouts: 22.9 us -> none  [the longest x2 5.44 us: per_device(): lax.all_to_all(jnp.stack((real_part, imag_part)), 'grid', split_axis=2, c...]
    all_to_all x1 -> x0, blocking collectives: 17.7 us -> none  [potential_split(): lax.all_to_all(jnp.stack((real_part, imag_part)), 'grid', split_axis=4, c...]
    all_to_all x4 -> x0, other arithmetic: 16.6 us -> none  [the longest x1 4.58 us: potential_split(): lax.all_to_all(jnp.stack((real_part, imag_part)), 'grid', split_axis=2, c...]
    squeeze x6 -> x0, local copies, waits for them, and re-layouts: 12.7 us -> none  [the longest x3 6.95 us: potential_split(): arrived[1]]
  transfers between devices with their start and end apart: 7 -> 6, of which waited for: 7 -> 6; matrix products, arithmetic and copies ran while one was open for 8% -> 1% of each run, Pallas kernels for 0% -> 4%
where the time goes in v1:
time: 356 us; the launch traced here: 355 us
  waiting for transfers between devices  273 us (77%)
  Pallas kernels  40.4 us (11%)
  starting transfers between devices  17 us (5%)
  between operations  14.8 us (4%)
  local copies, waits for them, and re-layouts  7.5 us (2%)
    reduce_scatter x1, waiting for transfers between devices, plane_potential(): lax.psum_scatter(partial_value, 'band', scatter_dimension=2, tiled=True)  91.5 us
    all_to_all x2, waiting for transfers between devices, per_device(): came.append(lax.all_to_all(sent, 'grid', 0, 0, tiled=True))  81.1 us
    all_gather x1, waiting for transfers between devices, plane_potential(): return lax.all_gather(potential_rows, 'band', axis=0, tiled=True)  70.7 us
    all_to_all x2, waiting for transfers between devices, plane_potential(): came = lax.all_to_all(sent.reshape(block), both, 0, 0, tiled=True)  29.3 us
    pallas_call x2, Pallas kernels, per_device(): pl.pallas_call(functools.partial(field_forward, length, rows, groups), gr...  18.6 us
    pallas_call x2, Pallas kernels, per_device(): pl.pallas_call(functools.partial(field_finish, length, rows, count), grid...  11.9 us
    all_to_all x2, starting transfers between devices, per_device(): came.append(lax.all_to_all(sent, 'grid', 0, 0, tiled=True))  9.7 us
    all_to_all x2, starting transfers between devices, plane_potential(): came = lax.all_to_all(sent.reshape(block), both, 0, 0, tiled=True)  7.21 us
  transfers between devices with their start and end apart: 6, of which 6 were waited for; matrix products, arithmetic and copies ran while one was open for 1% of the time, Pallas kernels for 4%

profile of v1, /device:TPU:0, one launch (start us, length us, event | category | flops | bytes accessed | tf_op | source)
XLA Modules:
  0.0 355.4 jit_solution(700857194677954502)
XLA Ops:
  7.2 1.6 convert.3
  9.8 2.6 copy.33
  12.5 91.5 %reduce-scatter.2.cloned.1.call-done = f32[2,32,16,128]{3,2,1,0:T(8,128)} async-done(((f32[2,32,128,128]{3,2,1,0:T(8,128)}), f32[2,32,16,128]{3,2,1,0:T(8,128)}) %reduce-scatter.2.cloned.1.call-update) | async-done | bytes 524304 | tf_op jit(solution)/shard_map/reduce_scatter | solution.py:267
  104.0 1.9 copy_bitcast_fusion.d_ref
  105.9 3.6 %shard_map.230 = f32[1024,128]{1,0:T(8,128)} custom-call(f32[4,2,128,128]{3,2,1,0:T(8,128)} %copy_bitcast_fusion.d_ref, bf16[256,256]{1,0:T(8,128)(2,1)} %constant.59.clone.zh.yh, bf16[256,256]{1,0:T(8,128)(2,1)} %constant.60.clone.zl.yl, bf16[256,256]{1,0:T(8,128)(2,1)} %constant.57.clone.yh.zh, bf16[256,256]{1,0:T(8,128)(2,1)} %constant.58.clone.yl.zl), custom_call_target="tpu_custom_call" | custom-call | flops 402653184 | bytes 2097152 | tf_op jit(solution)/shard_map/pallas_call | solution.py:286
  109.5 4.2 %all-to-all-start = ((f32[32,32,128]{2,1,0:T(8,128)}), f32[32,32,128]{2,1,0:T(8,128)S(1)}, u32[]{:S(2)}, u32[]{:S(2)}) async-start(f32[32,32,128]{2,1,0:T(8,128)} %bitcast.37), calls=%async_computation.1 | async-start | bytes 1048576 | tf_op jit(solution)/shard_map/all_to_all | solution.py:297
  114.1 0.8 divide_select_fusion.k_ref
  114.8 14.5 %all-to-all-done = f32[32,32,128]{2,1,0:T(8,128)S(1)} async-done(((f32[32,32,128]{2,1,0:T(8,128)}), f32[32,32,128]{2,1,0:T(8,128)S(1)}, u32[]{:S(2)}, u32[]{:S(2)}) %all-to-all-start) | async-done | bytes 524320 | tf_op jit(solution)/shard_map/all_to_all | solution.py:297
  129.4 0.8 copy-done.2
  130.2 2.8 shard_map.231
  133.0 3.0 all-to-all-start.1
  136.0 0.7 constant_dynamic-slice_fusion.a_ref
  136.7 14.8 %all-to-all-done.1 = f32[32,32,128]{2,1,0:T(8,128)S(1)} async-done(((f32[32,32,128]{2,1,0:T(8,128)}), f32[32,32,128]{2,1,0:T(8,128)S(1)}, u32[]{:S(2)}, u32[]{:S(2)}) %all-to-all-start.1) | async-done | bytes 524320 | tf_op jit(solution)/shard_map/all_to_all | solution.py:307
  151.6 0.8 copy-done.3
  152.4 3.5 shard_map.232
  156.5 70.7 %all-gather.2.cloned.1.call-done.p_ref = f32[32,2,128,128]{3,2,1,0:T(8,128)} async-done(((f32[4,2,128,128]{3,2,1,0:T(8,128)}), f32[32,2,128,128]{3,2,1,0:T(8,128)}) %all-gather.2.cloned.1.call-update) | async-done | bytes 4194320 | tf_op jit(solution)/shard_map/all_gather | solution.py:316
  227.2 9.3 %shard_map.234 = f32[4,4,2,256,128]{4,3,2,1,0:T(8,128)} custom-call(f32[1]{0:T(128)S(6)} %copy.42.e_ref, f32[32,2,128,128]{3,2,1,0:T(8,128)} %all-gather.2.cloned.1.call-done.p_ref, bf16[32,128,128]{2,1,0:T(8,128)(2,1)} %bitcast.34, bf16[2,32,128,128]{3,2,1,0:T(8,128)(2,1)} %bitcast.29, f32[32,128,128]{2,1,0:T(8,128)} %l_ref.3, ...), custom_call_target="tpu_custom_call" | custom-call | flops 2415919104 | bytes 16777216 | tf_op jit(solution)/shard_map/pallas_call | solution.py:362
  236.5 4.8 %all-to-all-start.3 = ((f32[4,4,2,256,128]{4,3,2,1,0:T(8,128)}), f32[4,4,2,256,128]{4,3,2,1,0:T(8,128)}, u32[]{:S(2)}, u32[]{:S(2)}) async-start(f32[4,4,2,256,128]{4,3,2,1,0:T(8,128)} %shard_map.234), calls=%async_computation.4 | async-start | bytes 8388608 | tf_op jit(solution)/shard_map/all_to_all | solution.py:383
  241.3 9.3 %shard_map.233 = f32[4,4,2,256,128]{4,3,2,1,0:T(8,128)} custom-call(f32[1]{0:T(128)S(6)} %copy.42.e_ref, f32[32,2,128,128]{3,2,1,0:T(8,128)} %all-gather.2.cloned.1.call-done.p_ref, bf16[32,128,128]{2,1,0:T(8,128)(2,1)} %bitcast.35, bf16[2,32,128,128]{3,2,1,0:T(8,128)(2,1)} %bitcast.30, f32[32,128,128]{2,1,0:T(8,128)} %l_ref.3, ...), custom_call_target="tpu_custom_call" | custom-call | flops 2415919104 | bytes 16777216 | tf_op jit(solution)/shard_map/pallas_call | solution.py:362
  250.7 38.9 %all-to-all-done.3.v_ref = f32[4,4,2,256,128]{4,3,2,1,0:T(8,128)} async-done(((f32[4,4,2,256,128]{4,3,2,1,0:T(8,128)}), f32[4,4,2,256,128]{4,3,2,1,0:T(8,128)}, u32[]{:S(2)}, u32[]{:S(2)}) %all-to-all-start.3) | async-done | bytes 4194336 | tf_op jit(solution)/shard_map/all_to_all | solution.py:383
  289.5 4.9 %all-to-all-start.2 = ((f32[4,4,2,256,128]{4,3,2,1,0:T(8,128)}), f32[4,4,2,256,128]{4,3,2,1,0:T(8,128)}, u32[]{:S(2)}, u32[]{:S(2)}) async-start(f32[4,4,2,256,128]{4,3,2,1,0:T(8,128)} %shard_map.233), calls=%async_computation.3 | async-start | bytes 8388608 | tf_op jit(solution)/shard_map/all_to_all | solution.py:383
  294.4 5.9 %shard_map.235 = (f32[2,1,32,128,128]{4,3,2,1,0:T(8,128)}, f32[2,1,32,128,128]{4,3,2,1,0:T(8,128)}) custom-call(f32[4,4,2,256,128]{4,3,2,1,0:T(8,128)} %all-to-all-done.3.v_ref, bf16[256,256]{1,0:T(8,128)(2,1)} %constant.67.clone.wh, bf16[256,256]{1,0:T(8,128)(2,1)} %constant.68.clone.wl), custom_call_target="tpu_custom_call" | custom-call | flops 1610612736 | bytes 33554432 | tf_op jit(solution)/shard_map/pallas_call | solution.py:392
  300.3 42.3 %all-to-all-done.2.v_ref = f32[4,4,2,256,128]{4,3,2,1,0:T(8,128)} async-done(((f32[4,4,2,256,128]{4,3,2,1,0:T(8,128)}), f32[4,4,2,256,128]{4,3,2,1,0:T(8,128)}, u32[]{:S(2)}, u32[]{:S(2)}) %all-to-all-start.2) | async-done | bytes 4194336 | tf_op jit(solution)/shard_map/all_to_all | solution.py:383
  342.6 5.9 %shard_map.236 = (f32[2,1,32,128,128]{4,3,2,1,0:T(8,128)}, f32[2,1,32,128,128]{4,3,2,1,0:T(8,128)}) custom-call(f32[4,4,2,256,128]{4,3,2,1,0:T(8,128)} %all-to-all-done.2.v_ref, bf16[256,256]{1,0:T(8,128)(2,1)} %constant.67.clone.wh, bf16[256,256]{1,0:T(8,128)(2,1)} %constant.68.clone.wl, ...), custom_call_target="tpu_custom_call", output_to_operand_aliasing={{0}: (3, {}), {1}: (4, {})} | custom-call | flops 1610612736 | bytes 33554432 | tf_op jit(solution)/shard_map/pallas_call | solution.py:392
  (16 shorter events, 1.4 us)
Async XLA Ops:
  7.2 128.8 %copy-start = (f32[32,128,128]{2,1,0:T(8,128)S(1)}, f32[32,128,128]{2,1,0:T(8,128)}, u32[]{:S(2)}) copy-start(f32[32,128,128]{2,1,0:T(8,128)} %param.25) | copy-start | bytes 6291460
  7.2 96.8 %reduce-scatter.2.cloned.1.call-start = ((), (), s32[]{:S(2)}) async-start(), calls=%async_computation.5 | async-start | bytes 4718592 | tf_op jit(solution)/shard_map/reduce_scatter | solution.py:267
  7.2 2.0 copy-start.1
  109.5 19.9 %all-to-all-start = ((f32[32,32,128]{2,1,0:T(8,128)}), f32[32,32,128]{2,1,0:T(8,128)S(1)}, u32[]{:S(2)}, u32[]{:S(2)}) async-start(f32[32,32,128]{2,1,0:T(8,128)} %bitcast.37), calls=%async_computation.1 | async-start | bytes 1048576 | tf_op jit(solution)/shard_map/all_to_all | solution.py:297
  129.4 0.8 copy-start.2
  133.0 18.6 %all-to-all-start.1 = ((f32[32,32,128]{2,1,0:T(8,128)}), f32[32,32,128]{2,1,0:T(8,128)S(1)}, u32[]{:S(2)}, u32[]{:S(2)}) async-start(f32[32,32,128]{2,1,0:T(8,128)} %bitcast.38), calls=%async_computation.2 | async-start | bytes 1048576 | tf_op jit(solution)/shard_map/all_to_all | solution.py:307
  135.9 91.3 %all-gather.2.cloned.1.call-start = ((), (), s32[]{:S(2)}) async-start(), calls=%async_computation.6 | async-start | bytes 4718592 | tf_op jit(solution)/shard_map/all_gather | solution.py:316
  151.6 0.8 copy-start.3
  236.5 53.1 %all-to-all-start.3 = ((f32[4,4,2,256,128]{4,3,2,1,0:T(8,128)}), f32[4,4,2,256,128]{4,3,2,1,0:T(8,128)}, u32[]{:S(2)}, u32[]{:S(2)}) async-start(f32[4,4,2,256,128]{4,3,2,1,0:T(8,128)} %shard_map.234), calls=%async_computation.4 | async-start | bytes 8388608 | tf_op jit(solution)/shard_map/all_to_all | solution.py:383
  289.5 53.1 %all-to-all-start.2 = ((f32[4,4,2,256,128]{4,3,2,1,0:T(8,128)}), f32[4,4,2,256,128]{4,3,2,1,0:T(8,128)}, u32[]{:S(2)}, u32[]{:S(2)}) async-start(f32[4,4,2,256,128]{4,3,2,1,0:T(8,128)} %shard_map.233), calls=%async_computation.3 | async-start | bytes 8388608 | tf_op jit(solution)/shard_map/all_to_all | solution.py:383
Sparse Core Ops, SparseCore 0:
  12.6 91.3 reduce-scatter.1
  156.0 71.1 all-gather.1

commit v2 on v1

--- a/solution.py
+++ b/solution.py
@@ -184,7 +184,7 @@
         spec = jnp.concatenate([spec[:length], spec[length:]], axis=1)
         spec = times(spec, zh[...], zl[...])
         for k in range(2):
-            out_ref[x, k] = (
+            out_ref[k, x] = (
                 spec[:, k * length : (k + 1) * length] + a_ref[x] * d_ref[x, k]
             )
 
@@ -251,6 +251,193 @@
     return jnp.where(squared > 0, scaled, 0.0)
 
 
+def peer(band):
+    return {"device_id": {"band": band}, "device_id_type": pl.DeviceIdType.MESH}
+
+
+def greet(bands):
+    barrier = pltpu.get_barrier_semaphore()
+    for band in bands:
+        pl.semaphore_signal(barrier, inc=1, **peer(band))
+    pl.semaphore_wait(barrier, len(bands))
+
+
+def remote(source, target, sends, receives, slot, band):
+    return pltpu.make_async_remote_copy(
+        src_ref=source,
+        dst_ref=target,
+        send_sem=sends.at[slot],
+        recv_sem=receives.at[slot],
+        **peer(band),
+    )
+
+
+def around(line, here, y):
+    near = [2 * here + 1 - y]
+    near += [2 * (here + 1) + y] if here + 1 < line else []
+    near += [2 * (here - 1) + y] if here > 0 else []
+    return near
+
+
+def reduce_planes(line, share, o_ref, t_ref, out_ref, part, across, up, down, *sems):
+    y_send, y_recv, up_send, up_recv, down_send, down_recv = sems
+    me = lax.axis_index("band")
+    y = lax.rem(me, 2)
+    count = share * 2
+
+    @pl.loop(0, 2 * line * share)
+    def _(x):
+        wide = 2.0 * o_ref[x].astype(f32)
+        for k in range(2):
+            part[x // share, lax.rem(x, share) * 2 + k] = wide * t_ref[k, x].astype(f32)
+
+    def role(here):
+        greet(around(line, here, y))
+        order = sorted(range(line), key=lambda j: (-abs(j - here), j < here))
+        copies = []
+        for j in order:
+            copy = remote(
+                part.at[2 * j + 1 - y], across.at[j], y_send, y_recv, j, 2 * here + 1 - y
+            )
+            copy.start()
+            copies.append(copy)
+        arrived = list(copies)
+        for j, copy in zip(order, arrived):
+            copy.wait_recv()
+            others = [across]
+            if j >= here and here > 0:
+                remote(part.at[0], up.at[j], up_send, up_recv, j, 2 * here + 1 - y).wait_recv()
+                others.append(up)
+            if j <= here and here + 1 < line:
+                remote(part.at[0], down.at[j], down_send, down_recv, j, 2 * here + 1 - y).wait_recv()
+                others.append(down)
+            mine = 2 * j + y
+
+            @pl.loop(0, count)
+            def _(i):
+                total = part[mine, i]
+                for other in others:
+                    total = total + other[j, i]
+                if j == here:
+                    out_ref[i] = total
+                else:
+                    part[mine, i] = total
+
+            if j > here:
+                copy = remote(part.at[mine], up.at[j], up_send, up_recv, j, 2 * here + 2 + y)
+            elif j < here:
+                copy = remote(
+                    part.at[mine], down.at[j], down_send, down_recv, j, 2 * here - 2 + y
+                )
+            if j != here:
+                copy.start()
+                copies.append(copy)
+        for copy in copies:
+            copy.wait_send()
+
+    for here in range(line):
+        pl.when(me // 2 == here)(functools.partial(role, here))
+
+
+def gather_planes(line, trial, p_ref, out_ref, held, *sems):
+    y_send, y_recv, up_send, up_recv, down_send, down_recv, out_sem = sems
+    me = lax.axis_index("band")
+    y = lax.rem(me, 2)
+
+    def role(here):
+        greet(around(line, here, y))
+        copies, outs = [], []
+
+        def keep(source, band, slot):
+            copy = pltpu.make_async_copy(source, out_ref.at[band], out_sem.at[slot])
+            copy.start()
+            outs.append(copy)
+
+        def spread(source, j, upward, downward):
+            band = 2 * j + y
+            if upward and here + 1 < line:
+                copies.append(
+                    remote(source, held.at[band], up_send, up_recv, j, 2 * here + 2 + y)
+                )
+                copies[-1].start()
+            if downward and here > 0:
+                copies.append(
+                    remote(source, held.at[band], down_send, down_recv, j, 2 * here - 2 + y)
+                )
+                copies[-1].start()
+            copies.append(
+                remote(source, held.at[band], y_send, y_recv, j, 2 * here + 1 - y)
+            )
+            copies[-1].start()
+            keep(source, band, 2 * j)
+
+        spread(p_ref.at[trial], here, True, True)
+        order = [here]
+        for far in range(1, line):
+            for j, sends, receives in (
+                (here - far, up_send, up_recv),
+                (here + far, down_send, down_recv),
+            ):
+                if 0 <= j < line:
+                    block = held.at[2 * j + y]
+                    remote(block, block, sends, receives, j, 2 * here + 1 - y).wait_recv()
+                    spread(block, j, j < here, j > here)
+                    order.append(j)
+        for j in order:
+            block = held.at[2 * j + 1 - y]
+            remote(block, block, y_send, y_recv, j, 2 * here + 1 - y).wait_recv()
+            keep(block, 2 * j + 1 - y, 2 * j + 1)
+        for copy in copies:
+            copy.wait_send()
+        for copy in outs:
+            copy.wait()
+
+    for here in range(line):
+        pl.when(me // 2 == here)(functools.partial(role, here))
+
+
+def reduced(bands, orbital, trial):
+    length, x_here = orbital.shape[1], orbital.shape[0]
+    share, line = x_here // bands, bands // 2
+    block = (share * 2, length, length)
+    dma = pltpu.SemaphoreType.DMA((line,))
+    out = pl.pallas_call(
+        functools.partial(reduce_planes, line, share),
+        out_shape=jax.ShapeDtypeStruct(block, f32),
+        in_specs=whole_spec(2),
+        out_specs=whole_spec(1)[0],
+        scratch_shapes=[pltpu.VMEM((bands, *block), f32)]
+        + [pltpu.VMEM((line, *block), f32)] * 3
+        + [dma] * 6,
+        compiler_params=pltpu.CompilerParams(
+            vmem_limit_bytes=vmem_grant, collective_id=1, has_side_effects=True
+        ),
+        cost_estimate=cost(share * length**3, 30 * x_here * length**2 * 4),
+    )(orbital, trial)
+    return out.reshape(share, 2, length, length)
+
+
+def gathered(bands, trial, rows):
+    share, length = rows.shape[1], rows.shape[2]
+    line = bands // 2
+    dma = pltpu.SemaphoreType.DMA((line,))
+    block = (bands, share, length, length)
+    out = pl.pallas_call(
+        functools.partial(gather_planes, line, trial),
+        out_shape=jax.ShapeDtypeStruct(block, f32),
+        in_specs=whole_spec(1),
+        out_specs=pl.BlockSpec(memory_space=pl.ANY),
+        scratch_shapes=[pltpu.VMEM(block, f32)]
+        + [dma] * 6
+        + [pltpu.SemaphoreType.DMA((bands,))],
+        compiler_params=pltpu.CompilerParams(
+            vmem_limit_bytes=vmem_grant, collective_id=2 + trial, has_side_effects=True
+        ),
+        cost_estimate=cost(share * length**3, 30 * bands * share * length**2 * 4),
+    )(rows)
+    return out.reshape(bands * share, length, length)
+
+
 def plane_potential(bands, groups, orbital, trial, alda_kernel):
     length, x_here = orbital.shape[1], orbital.shape[0]
     share = x_here // bands
@@ -261,11 +448,7 @@
     bs = length // devices
     unit = 2 * length**3
 
-    partial_value = 2.0 * (trial.astype(f32) * orbital.astype(f32)[None])
-    partial_value = partial_value.reshape(2, bands, share * length // 16, 16, length)
-    partial_value = partial_value.swapaxes(1, 2).reshape(2, -1, bands * 16, length)
-    density = lax.psum_scatter(partial_value, "band", scatter_dimension=2, tiled=True)
-    density = density.reshape(2, share, length, length).transpose(1, 0, 2, 3)
+    density = reduced(bands, orbital, trial)
     alda_rows = lax.dynamic_slice_in_dim(
         alda_kernel, lax.axis_index("band") * share, share, 0
     )
@@ -307,13 +490,13 @@
     came = lax.all_to_all(sent.reshape(block), both, 0, 0, tiled=True)
     potential_rows = pl.pallas_call(
         functools.partial(plane_backward, length, share),
-        out_shape=jax.ShapeDtypeStruct(density.shape, f32),
+        out_shape=jax.ShapeDtypeStruct((2, share, length, length), f32),
         in_specs=whole_spec(7),
         out_specs=whole_spec(1)[0],
         compiler_params=params,
         cost_estimate=cost(24 * share * unit, 8 * share * length**2 * 4),
     )(came.reshape(flat), density, alda_rows, *bwd_left, *bwd_right)
-    return lax.all_gather(potential_rows, "band", axis=0, tiled=True)
+    return [gathered(bands, k, potential_rows) for k in range(2)]
 
 
 def pencil_potential(orbital, trial, alda_kernel):
@@ -329,7 +512,7 @@
     potential = lax.all_gather(
         hartree + alda_rows[None] * density, "band", axis=2, tiled=True
     )
-    return potential.transpose(1, 0, 2, 3)
+    return [potential[k] for k in range(trial.shape[0])]
 
 
 def per_device(bands, groups, orbitals, trial_vectors, alda_kernel, local_potential, band_energies):
@@ -340,7 +523,12 @@
     unit = 2 * length**3
     forward = right_block(length, -1.0)
     fwd_left = halves(forward.T)
-    if x_here % bands == 0 and length % (bands * groups) == 0 and trial.shape[0] == 2:
+    if (
+        bands % 2 == 0
+        and x_here % bands == 0
+        and length % (bands * groups) == 0
+        and trial.shape[0] == 2
+    ):
         potential = plane_potential(bands, groups, orbital, trial, alda_kernel)
     else:
         potential = pencil_potential(orbital, trial, alda_kernel)
@@ -365,7 +553,7 @@
             out_shape=jax.ShapeDtypeStruct((groups, steps, 2, width * rows, length), f32),
             in_specs=[
                 pl.BlockSpec(memory_space=pltpu.SMEM),
-                pl.BlockSpec((rows, squeezed, length, length), lambda i, k=k: (i, k, 0, 0)),
+                pl.BlockSpec(cube, lambda i: (i, 0, 0)),
                 pl.BlockSpec(cube, lambda i: (i, 0, 0)),
                 pl.BlockSpec((squeezed, *cube), lambda i, k=k: (k, i, 0, 0)),
                 pl.BlockSpec(cube, lambda i: (i, 0, 0)),
@@ -379,7 +567,7 @@
             ),
             compiler_params=params,
             cost_estimate=cost(18 * x_here * unit, 8 * x_here * length**2 * 4),
-        )(band_energies, potential, orbital, trial, local_potential, *z_table, *fwd_left)
+        )(band_energies, potential[k], orbital, trial, local_potential, *z_table, *fwd_left)
         came.append(lax.all_to_all(sent, "grid", 0, 0, tiled=True))
 
     count = 8

time: 356 us -> 256 us (0.72)
  waiting for transfers between devices: 273 us -> 77.5 us
  Pallas kernels: 40.4 us -> 156 us
  between operations: 14.8 us -> 1.39 us
  local copies, waits for them, and re-layouts: 7.5 us -> 2.52 us
    pallas_call x0 -> x3, Pallas kernels: none -> 116 us  [the longest x2 60.7 us: gathered(): pl.pallas_call(functools.partial(gather_planes, line, trial), out_shape=j...]
    reduce_scatter x1 -> x0, waiting for transfers between devices: 91.5 us -> none  [plane_potential(): lax.psum_scatter(partial_value, 'band', scatter_dimension=2, tiled=True)]
    all_gather x1 -> x0, waiting for transfers between devices: 70.7 us -> none  [plane_potential(): return lax.all_gather(potential_rows, 'band', axis=0, tiled=True)]
    all_to_all x2, waiting for transfers between devices: 81.1 us -> 48.7 us  [per_device(): came.append(lax.all_to_all(sent, 'grid', 0, 0, tiled=True))]
    transpose x2 -> x0, local copies, waits for them, and re-layouts: 4.5 us -> none  [the longest x1 2.63 us: plane_potential(): partial_value.swapaxes(1, 2).reshape(2, -1, bands * 16, length)]
  transfers between devices with their start and end apart: 6 -> 4, of which waited for: 6 -> 4; matrix products, arithmetic and copies ran while one was open for 1% -> 1% of each run, Pallas kernels for 4% -> 19%
where the time goes in v2:
time: 256 us; the launch traced here: 255 us
  Pallas kernels  156 us (61%)
  waiting for transfers between devices  77.5 us (30%)
  starting transfers between devices  16.5 us (6%)
    pallas_call x2, Pallas kernels, gathered(): pl.pallas_call(functools.partial(gather_planes, line, trial), out_shape=j...  60.7 us
    pallas_call x1, Pallas kernels, reduced(): pl.pallas_call(functools.partial(reduce_planes, line, share), out_shape=j...  55.2 us
    all_to_all x2, waiting for transfers between devices, per_device(): came.append(lax.all_to_all(sent, 'grid', 0, 0, tiled=True))  48.7 us
    all_to_all x2, waiting for transfers between devices, plane_potential(): came = lax.all_to_all(sent.reshape(block), both, 0, 0, tiled=True)  28.8 us
    pallas_call x2, Pallas kernels, per_device(): pl.pallas_call(functools.partial(field_forward, length, rows, groups), gr...  18.8 us
    pallas_call x2, Pallas kernels, per_device(): pl.pallas_call(functools.partial(field_finish, length, rows, count), grid...  11.9 us
    all_to_all x2, starting transfers between devices, per_device(): came.append(lax.all_to_all(sent, 'grid', 0, 0, tiled=True))  9.77 us
    all_to_all x2, starting transfers between devices, plane_potential(): came = lax.all_to_all(sent.reshape(block), both, 0, 0, tiled=True)  6.72 us
  transfers between devices with their start and end apart: 4, of which 4 were waited for; matrix products, arithmetic and copies ran while one was open for 1% of the time, Pallas kernels for 19%

profile of v2, /device:TPU:0, one launch (start us, length us, event | category | flops | bytes accessed | tf_op | source)
XLA Modules:
  0.0 255.2 jit_solution(2327845881265886239)
XLA Ops:
  0.6 55.2 %shard_map.230 = f32[8,128,128]{2,1,0:T(8,128)} custom-call(bf16[32,128,128]{2,1,0:T(8,128)(2,1)} %bitcast.19, bf16[2,32,128,128]{3,2,1,0:T(8,128)(2,1)} %bitcast.16), custom_call_target="tpu_custom_call" | custom-call | flops 8388608 | bytes 62914560 | tf_op jit(solution)/shard_map/pallas_call | solution.py:404
  55.8 3.6 %shard_map.231 = f32[1024,128]{1,0:T(8,128)} custom-call(f32[4,2,128,128]{3,2,1,0:T(8,128)} %bitcast.24, bf16[256,256]{1,0:T(8,128)(2,1)} %constant.57.clone.zh.yh, bf16[256,256]{1,0:T(8,128)(2,1)} %constant.58.clone.zl.yl, bf16[256,256]{1,0:T(8,128)(2,1)} %constant.55.clone.yh.zh, bf16[256,256]{1,0:T(8,128)(2,1)} %constant.56.clone.yl.zl), custom_call_target="tpu_custom_call" | custom-call | flops 402653184 | bytes 2097152 | tf_op jit(solution)/shard_map/pallas_call | solution.py:469
  59.4 3.7 %all-to-all-start = ((f32[32,32,128]{2,1,0:T(8,128)}), f32[32,32,128]{2,1,0:T(8,128)S(1)}, u32[]{:S(2)}, u32[]{:S(2)}) async-start(f32[32,32,128]{2,1,0:T(8,128)} %bitcast.27), calls=%async_computation | async-start | bytes 1048576 | tf_op jit(solution)/shard_map/all_to_all | solution.py:480
  63.2 0.1 broadcast_add_fusion
  63.3 0.2 add.74
  63.5 0.8 divide_select_fusion.k_ref
  64.3 14.5 %all-to-all-done = f32[32,32,128]{2,1,0:T(8,128)S(1)} async-done(((f32[32,32,128]{2,1,0:T(8,128)}), f32[32,32,128]{2,1,0:T(8,128)S(1)}, u32[]{:S(2)}, u32[]{:S(2)}) %all-to-all-start) | async-done | bytes 524320 | tf_op jit(solution)/shard_map/all_to_all | solution.py:480
  78.8 0.8 copy-done.1
  79.6 2.8 %shard_map.232 = f32[32,4,8,128]{3,2,1,0:T(8,128)} custom-call(f32[32,4,8,128]{3,2,1,0:T(8,128)} %bitcast.26, f32[128,512]{1,0:T(8,128)} %divide_select_fusion.k_ref, bf16[256,256]{1,0:T(8,128)(2,1)} %constant.59.clone.fh, bf16[256,256]{1,0:T(8,128)(2,1)} %constant.60.clone.fl, bf16[256,256]{1,0:T(8,128)(2,1)} %constant.61.clone.ih, ...), custom_call_target="tpu_custom_call" | custom-call | flops 402653184 | bytes 2097152 | tf_op jit(solution)/shard_map/pallas_call | solution.py:482
  82.4 3.0 %all-to-all-start.1 = ((f32[32,32,128]{2,1,0:T(8,128)}), f32[32,32,128]{2,1,0:T(8,128)S(1)}, u32[]{:S(2)}, u32[]{:S(2)}) async-start(f32[32,32,128]{2,1,0:T(8,128)} %bitcast.28), calls=%async_computation.1 | async-start | bytes 1048576 | tf_op jit(solution)/shard_map/all_to_all | solution.py:490
  86.0 0.7 constant_dynamic-slice_fusion.a_ref
  86.8 14.2 %all-to-all-done.1 = f32[32,32,128]{2,1,0:T(8,128)S(1)} async-done(((f32[32,32,128]{2,1,0:T(8,128)}), f32[32,32,128]{2,1,0:T(8,128)S(1)}, u32[]{:S(2)}, u32[]{:S(2)}) %all-to-all-start.1) | async-done | bytes 524320 | tf_op jit(solution)/shard_map/all_to_all | solution.py:490
  101.0 0.8 copy-done.2
  101.8 3.5 %shard_map.233.p_ref = f32[2,4,128,128]{3,2,1,0:T(8,128)} custom-call(f32[1024,128]{1,0:T(8,128)} %bitcast.29, f32[4,2,128,128]{3,2,1,0:T(8,128)} %bitcast.25, f32[4,128,128]{2,1,0:T(8,128)} %constant_dynamic-slice_fusion.a_ref, bf16[256,256]{1,0:T(8,128)(2,1)} %constant.57.clone.zh.yh, bf16[256,256]{1,0:T(8,128)(2,1)} %constant.58.clone.zl.yl, ...), custom_call_target="tpu_custom_call" | custom-call | flops 402653184 | bytes 2097152 | tf_op jit(solution)/shard_map/pallas_call | solution.py:491
  105.3 28.4 %shard_map.236 = f32[8,4,128,128]{3,2,1,0:T(8,128)} custom-call(f32[2,4,128,128]{3,2,1,0:T(8,128)} %shard_map.233.p_ref), custom_call_target="tpu_custom_call" | custom-call | flops 8388608 | bytes 62914560 | tf_op jit(solution)/shard_map/pallas_call | solution.py:425
  133.7 9.4 %shard_map.237 = f32[4,4,2,256,128]{4,3,2,1,0:T(8,128)} custom-call(f32[1]{0:T(128)S(6)} %copy.33.e_ref, f32[32,128,128]{2,1,0:T(8,128)} %bitcast.23, bf16[32,128,128]{2,1,0:T(8,128)(2,1)} %bitcast.20, bf16[2,32,128,128]{3,2,1,0:T(8,128)(2,1)} %bitcast.17, f32[32,128,128]{2,1,0:T(8,128)} %l_ref.3, bf16[128,256]{1,0:T(8,128)(2,1)} %constant.63.clone.zh, ...), custom_call_target="tpu_custom_call" | custom-call | flops 2415919104 | bytes 16777216 | tf_op jit(solution)/shard_map/pallas_call | solution.py:550
  143.1 4.8 %all-to-all-start.3 = ((f32[4,4,2,256,128]{4,3,2,1,0:T(8,128)}), f32[4,4,2,256,128]{4,3,2,1,0:T(8,128)}, u32[]{:S(2)}, u32[]{:S(2)}) async-start(f32[4,4,2,256,128]{4,3,2,1,0:T(8,128)} %shard_map.237), calls=%async_computation.3 | async-start | bytes 8388608 | tf_op jit(solution)/shard_map/all_to_all | solution.py:571
  147.9 32.3 %shard_map.234 = f32[8,4,128,128]{3,2,1,0:T(8,128)} custom-call(f32[2,4,128,128]{3,2,1,0:T(8,128)} %shard_map.233.p_ref), custom_call_target="tpu_custom_call" | custom-call | flops 8388608 | bytes 62914560 | tf_op jit(solution)/shard_map/pallas_call | solution.py:425
  180.2 9.4 %shard_map.235 = f32[4,4,2,256,128]{4,3,2,1,0:T(8,128)} custom-call(f32[1]{0:T(128)S(6)} %copy.33.e_ref, f32[32,128,128]{2,1,0:T(8,128)} %bitcast.22, bf16[32,128,128]{2,1,0:T(8,128)(2,1)} %bitcast.21, bf16[2,32,128,128]{3,2,1,0:T(8,128)(2,1)} %bitcast.18, f32[32,128,128]{2,1,0:T(8,128)} %l_ref.3, bf16[128,256]{1,0:T(8,128)(2,1)} %constant.63.clone.zh, ...), custom_call_target="tpu_custom_call" | custom-call | flops 2415919104 | bytes 16777216 | tf_op jit(solution)/shard_map/pallas_call | solution.py:550
  189.6 6.5 %all-to-all-done.3.v_ref = f32[4,4,2,256,128]{4,3,2,1,0:T(8,128)} async-done(((f32[4,4,2,256,128]{4,3,2,1,0:T(8,128)}), f32[4,4,2,256,128]{4,3,2,1,0:T(8,128)}, u32[]{:S(2)}, u32[]{:S(2)}) %all-to-all-start.3) | async-done | bytes 4194336 | tf_op jit(solution)/shard_map/all_to_all | solution.py:571
  196.1 4.9 %all-to-all-start.2 = ((f32[4,4,2,256,128]{4,3,2,1,0:T(8,128)}), f32[4,4,2,256,128]{4,3,2,1,0:T(8,128)}, u32[]{:S(2)}, u32[]{:S(2)}) async-start(f32[4,4,2,256,128]{4,3,2,1,0:T(8,128)} %shard_map.235), calls=%async_computation.2 | async-start | bytes 8388608 | tf_op jit(solution)/shard_map/all_to_all | solution.py:571
  201.1 5.9 %shard_map.238 = (f32[2,1,32,128,128]{4,3,2,1,0:T(8,128)}, f32[2,1,32,128,128]{4,3,2,1,0:T(8,128)}) custom-call(f32[4,4,2,256,128]{4,3,2,1,0:T(8,128)} %all-to-all-done.3.v_ref, bf16[256,256]{1,0:T(8,128)(2,1)} %constant.65.clone.wh, bf16[256,256]{1,0:T(8,128)(2,1)} %constant.66.clone.wl), custom_call_target="tpu_custom_call" | custom-call | flops 1610612736 | bytes 33554432 | tf_op jit(solution)/shard_map/pallas_call | solution.py:580
  207.0 42.3 %all-to-all-done.2.v_ref = f32[4,4,2,256,128]{4,3,2,1,0:T(8,128)} async-done(((f32[4,4,2,256,128]{4,3,2,1,0:T(8,128)}), f32[4,4,2,256,128]{4,3,2,1,0:T(8,128)}, u32[]{:S(2)}, u32[]{:S(2)}) %all-to-all-start.2) | async-done | bytes 4194336 | tf_op jit(solution)/shard_map/all_to_all | solution.py:571
  249.2 5.9 %shard_map.239 = (f32[2,1,32,128,128]{4,3,2,1,0:T(8,128)}, f32[2,1,32,128,128]{4,3,2,1,0:T(8,128)}) custom-call(f32[4,4,2,256,128]{4,3,2,1,0:T(8,128)} %all-to-all-done.2.v_ref, bf16[256,256]{1,0:T(8,128)(2,1)} %constant.65.clone.wh, bf16[256,256]{1,0:T(8,128)(2,1)} %constant.66.clone.wl, ...), custom_call_target="tpu_custom_call", output_to_operand_aliasing={{0}: (3, {}), {1}: (4, {})} | custom-call | flops 1610612736 | bytes 33554432 | tf_op jit(solution)/shard_map/pallas_call | solution.py:580
  (7 shorter events, 0.0 us)
Async XLA Ops:
  0.6 85.4 %copy-start = (f32[32,128,128]{2,1,0:T(8,128)S(1)}, f32[32,128,128]{2,1,0:T(8,128)}, u32[]{:S(2)}) copy-start(f32[32,128,128]{2,1,0:T(8,128)} %param.25) | copy-start | bytes 6291460
  59.4 19.4 %all-to-all-start = ((f32[32,32,128]{2,1,0:T(8,128)}), f32[32,32,128]{2,1,0:T(8,128)S(1)}, u32[]{:S(2)}, u32[]{:S(2)}) async-start(f32[32,32,128]{2,1,0:T(8,128)} %bitcast.27), calls=%async_computation | async-start | bytes 1048576 | tf_op jit(solution)/shard_map/all_to_all | solution.py:480
  78.8 0.8 copy-start.1
  82.4 18.6 %all-to-all-start.1 = ((f32[32,32,128]{2,1,0:T(8,128)}), f32[32,32,128]{2,1,0:T(8,128)S(1)}, u32[]{:S(2)}, u32[]{:S(2)}) async-start(f32[32,32,128]{2,1,0:T(8,128)} %bitcast.28), calls=%async_computation.1 | async-start | bytes 1048576 | tf_op jit(solution)/shard_map/all_to_all | solution.py:490
  101.0 0.8 copy-start.2
  143.1 53.0 %all-to-all-start.3 = ((f32[4,4,2,256,128]{4,3,2,1,0:T(8,128)}), f32[4,4,2,256,128]{4,3,2,1,0:T(8,128)}, u32[]{:S(2)}, u32[]{:S(2)}) async-start(f32[4,4,2,256,128]{4,3,2,1,0:T(8,128)} %shard_map.237), calls=%async_computation.3 | async-start | bytes 8388608 | tf_op jit(solution)/shard_map/all_to_all | solution.py:571
  196.1 53.1 %all-to-all-start.2 = ((f32[4,4,2,256,128]{4,3,2,1,0:T(8,128)}), f32[4,4,2,256,128]{4,3,2,1,0:T(8,128)}, u32[]{:S(2)}, u32[]{:S(2)}) async-start(f32[4,4,2,256,128]{4,3,2,1,0:T(8,128)} %shard_map.235), calls=%async_computation.2 | async-start | bytes 8388608 | tf_op jit(solution)/shard_map/all_to_all | solution.py:571

commit v3 on v2

--- a/solution.py
+++ b/solution.py
@@ -285,22 +285,29 @@
     y = lax.rem(me, 2)
     count = share * 2
 
-    @pl.loop(0, 2 * line * share)
-    def _(x):
-        wide = 2.0 * o_ref[x].astype(f32)
-        for k in range(2):
-            part[x // share, lax.rem(x, share) * 2 + k] = wide * t_ref[k, x].astype(f32)
+    def product(block):
+        @pl.loop(0, share)
+        def _(i):
+            x = block * share + i
+            wide = 2.0 * o_ref[x].astype(f32)
+            for k in range(2):
+                part[block, 2 * i + k] = wide * t_ref[k, x].astype(f32)
 
     def role(here):
-        greet(around(line, here, y))
         order = sorted(range(line), key=lambda j: (-abs(j - here), j < here))
         copies = []
-        for j in order:
+        blocks = [2 * j + 1 - y for j in order] + [2 * j + y for j in order]
+        product(blocks[0])
+        greet(around(line, here, y))
+        for turn, j in enumerate(order):
+            product(blocks[turn + 1])
             copy = remote(
                 part.at[2 * j + 1 - y], across.at[j], y_send, y_recv, j, 2 * here + 1 - y
             )
             copy.start()
             copies.append(copy)
+        for block in blocks[line + 1 :]:
+            product(block)
         arrived = list(copies)
         for j, copy in zip(order, arrived):
             copy.wait_recv()

time: 256 us -> 256 us (level)
  no operation moved by 1% of the time
where the time goes in v3:
time: 256 us; the launch traced here: 255 us
  Pallas kernels  156 us (61%)
  waiting for transfers between devices  77.5 us (30%)
  starting transfers between devices  16.5 us (6%)
    pallas_call x2, Pallas kernels, gathered(): pl.pallas_call(functools.partial(gather_planes, line, trial), out_shape=j...  60.7 us
    pallas_call x1, Pallas kernels, reduced(): pl.pallas_call(functools.partial(reduce_planes, line, share), out_shape=j...  54.7 us
    all_to_all x2, waiting for transfers between devices, per_device(): came.append(lax.all_to_all(sent, 'grid', 0, 0, tiled=True))  48.7 us
    all_to_all x2, waiting for transfers between devices, plane_potential(): came = lax.all_to_all(sent.reshape(block), both, 0, 0, tiled=True)  28.8 us
    pallas_call x2, Pallas kernels, per_device(): pl.pallas_call(functools.partial(field_forward, length, rows, groups), gr...  18.8 us
    pallas_call x2, Pallas kernels, per_device(): pl.pallas_call(functools.partial(field_finish, length, rows, count), grid...  11.9 us
    all_to_all x2, starting transfers between devices, per_device(): came.append(lax.all_to_all(sent, 'grid', 0, 0, tiled=True))  9.77 us
    all_to_all x2, starting transfers between devices, plane_potential(): came = lax.all_to_all(sent.reshape(block), both, 0, 0, tiled=True)  6.71 us
  transfers between devices with their start and end apart: 4, of which 4 were waited for; matrix products, arithmetic and copies ran while one was open for 1% of the time, Pallas kernels for 19%

profile of v3, /device:TPU:0, one launch (start us, length us, event | category | flops | bytes accessed | tf_op | source)
XLA Modules:
  0.0 254.7 jit_solution(16542021865520172335)
XLA Ops:
  0.6 54.7 %shard_map.230 = f32[8,128,128]{2,1,0:T(8,128)} custom-call(bf16[32,128,128]{2,1,0:T(8,128)(2,1)} %bitcast.19, bf16[2,32,128,128]{3,2,1,0:T(8,128)(2,1)} %bitcast.16), custom_call_target="tpu_custom_call" | custom-call | flops 8388608 | bytes 62914560 | tf_op jit(solution)/shard_map/pallas_call | solution.py:411
  55.4 3.6 %shard_map.231 = f32[1024,128]{1,0:T(8,128)} custom-call(f32[4,2,128,128]{3,2,1,0:T(8,128)} %bitcast.24, bf16[256,256]{1,0:T(8,128)(2,1)} %constant.57.clone.zh.yh, bf16[256,256]{1,0:T(8,128)(2,1)} %constant.58.clone.zl.yl, bf16[256,256]{1,0:T(8,128)(2,1)} %constant.55.clone.yh.zh, bf16[256,256]{1,0:T(8,128)(2,1)} %constant.56.clone.yl.zl), custom_call_target="tpu_custom_call" | custom-call | flops 402653184 | bytes 2097152 | tf_op jit(solution)/shard_map/pallas_call | solution.py:476
  59.0 3.7 %all-to-all-start = ((f32[32,32,128]{2,1,0:T(8,128)}), f32[32,32,128]{2,1,0:T(8,128)S(1)}, u32[]{:S(2)}, u32[]{:S(2)}) async-start(f32[32,32,128]{2,1,0:T(8,128)} %bitcast.27), calls=%async_computation | async-start | bytes 1048576 | tf_op jit(solution)/shard_map/all_to_all | solution.py:487
  62.8 0.1 broadcast_add_fusion
  62.9 0.2 add.74
  63.1 0.8 divide_select_fusion.k_ref
  63.8 14.5 %all-to-all-done = f32[32,32,128]{2,1,0:T(8,128)S(1)} async-done(((f32[32,32,128]{2,1,0:T(8,128)}), f32[32,32,128]{2,1,0:T(8,128)S(1)}, u32[]{:S(2)}, u32[]{:S(2)}) %all-to-all-start) | async-done | bytes 524320 | tf_op jit(solution)/shard_map/all_to_all | solution.py:487
  78.4 0.8 copy-done.1
  79.2 2.8 %shard_map.232 = f32[32,4,8,128]{3,2,1,0:T(8,128)} custom-call(f32[32,4,8,128]{3,2,1,0:T(8,128)} %bitcast.26, f32[128,512]{1,0:T(8,128)} %divide_select_fusion.k_ref, bf16[256,256]{1,0:T(8,128)(2,1)} %constant.59.clone.fh, bf16[256,256]{1,0:T(8,128)(2,1)} %constant.60.clone.fl, bf16[256,256]{1,0:T(8,128)(2,1)} %constant.61.clone.ih, ...), custom_call_target="tpu_custom_call" | custom-call | flops 402653184 | bytes 2097152 | tf_op jit(solution)/shard_map/pallas_call | solution.py:489
  82.0 3.0 %all-to-all-start.1 = ((f32[32,32,128]{2,1,0:T(8,128)}), f32[32,32,128]{2,1,0:T(8,128)S(1)}, u32[]{:S(2)}, u32[]{:S(2)}) async-start(f32[32,32,128]{2,1,0:T(8,128)} %bitcast.28), calls=%async_computation.1 | async-start | bytes 1048576 | tf_op jit(solution)/shard_map/all_to_all | solution.py:497
  85.6 0.7 constant_dynamic-slice_fusion.a_ref
  86.3 14.2 %all-to-all-done.1 = f32[32,32,128]{2,1,0:T(8,128)S(1)} async-done(((f32[32,32,128]{2,1,0:T(8,128)}), f32[32,32,128]{2,1,0:T(8,128)S(1)}, u32[]{:S(2)}, u32[]{:S(2)}) %all-to-all-start.1) | async-done | bytes 524320 | tf_op jit(solution)/shard_map/all_to_all | solution.py:497
  100.6 0.8 copy-done.2
  101.4 3.5 %shard_map.233.p_ref = f32[2,4,128,128]{3,2,1,0:T(8,128)} custom-call(f32[1024,128]{1,0:T(8,128)} %bitcast.29, f32[4,2,128,128]{3,2,1,0:T(8,128)} %bitcast.25, f32[4,128,128]{2,1,0:T(8,128)} %constant_dynamic-slice_fusion.a_ref, bf16[256,256]{1,0:T(8,128)(2,1)} %constant.57.clone.zh.yh, bf16[256,256]{1,0:T(8,128)(2,1)} %constant.58.clone.zl.yl, ...), custom_call_target="tpu_custom_call" | custom-call | flops 402653184 | bytes 2097152 | tf_op jit(solution)/shard_map/pallas_call | solution.py:498
  104.9 28.4 %shard_map.236 = f32[8,4,128,128]{3,2,1,0:T(8,128)} custom-call(f32[2,4,128,128]{3,2,1,0:T(8,128)} %shard_map.233.p_ref), custom_call_target="tpu_custom_call" | custom-call | flops 8388608 | bytes 62914560 | tf_op jit(solution)/shard_map/pallas_call | solution.py:432
  133.2 9.4 %shard_map.237 = f32[4,4,2,256,128]{4,3,2,1,0:T(8,128)} custom-call(f32[1]{0:T(128)S(6)} %copy.33.e_ref, f32[32,128,128]{2,1,0:T(8,128)} %bitcast.23, bf16[32,128,128]{2,1,0:T(8,128)(2,1)} %bitcast.20, bf16[2,32,128,128]{3,2,1,0:T(8,128)(2,1)} %bitcast.17, f32[32,128,128]{2,1,0:T(8,128)} %l_ref.3, bf16[128,256]{1,0:T(8,128)(2,1)} %constant.63.clone.zh, ...), custom_call_target="tpu_custom_call" | custom-call | flops 2415919104 | bytes 16777216 | tf_op jit(solution)/shard_map/pallas_call | solution.py:557
  142.6 4.8 %all-to-all-start.3 = ((f32[4,4,2,256,128]{4,3,2,1,0:T(8,128)}), f32[4,4,2,256,128]{4,3,2,1,0:T(8,128)}, u32[]{:S(2)}, u32[]{:S(2)}) async-start(f32[4,4,2,256,128]{4,3,2,1,0:T(8,128)} %shard_map.237), calls=%async_computation.3 | async-start | bytes 8388608 | tf_op jit(solution)/shard_map/all_to_all | solution.py:578
  147.5 32.3 %shard_map.234 = f32[8,4,128,128]{3,2,1,0:T(8,128)} custom-call(f32[2,4,128,128]{3,2,1,0:T(8,128)} %shard_map.233.p_ref), custom_call_target="tpu_custom_call" | custom-call | flops 8388608 | bytes 62914560 | tf_op jit(solution)/shard_map/pallas_call | solution.py:432
  179.8 9.4 %shard_map.235 = f32[4,4,2,256,128]{4,3,2,1,0:T(8,128)} custom-call(f32[1]{0:T(128)S(6)} %copy.33.e_ref, f32[32,128,128]{2,1,0:T(8,128)} %bitcast.22, bf16[32,128,128]{2,1,0:T(8,128)(2,1)} %bitcast.21, bf16[2,32,128,128]{3,2,1,0:T(8,128)(2,1)} %bitcast.18, f32[32,128,128]{2,1,0:T(8,128)} %l_ref.3, bf16[128,256]{1,0:T(8,128)(2,1)} %constant.63.clone.zh, ...), custom_call_target="tpu_custom_call" | custom-call | flops 2415919104 | bytes 16777216 | tf_op jit(solution)/shard_map/pallas_call | solution.py:557
  189.2 6.5 %all-to-all-done.3.v_ref = f32[4,4,2,256,128]{4,3,2,1,0:T(8,128)} async-done(((f32[4,4,2,256,128]{4,3,2,1,0:T(8,128)}), f32[4,4,2,256,128]{4,3,2,1,0:T(8,128)}, u32[]{:S(2)}, u32[]{:S(2)}) %all-to-all-start.3) | async-done | bytes 4194336 | tf_op jit(solution)/shard_map/all_to_all | solution.py:578
  195.7 4.9 %all-to-all-start.2 = ((f32[4,4,2,256,128]{4,3,2,1,0:T(8,128)}), f32[4,4,2,256,128]{4,3,2,1,0:T(8,128)}, u32[]{:S(2)}, u32[]{:S(2)}) async-start(f32[4,4,2,256,128]{4,3,2,1,0:T(8,128)} %shard_map.235), calls=%async_computation.2 | async-start | bytes 8388608 | tf_op jit(solution)/shard_map/all_to_all | solution.py:578
  200.6 5.9 %shard_map.238 = (f32[2,1,32,128,128]{4,3,2,1,0:T(8,128)}, f32[2,1,32,128,128]{4,3,2,1,0:T(8,128)}) custom-call(f32[4,4,2,256,128]{4,3,2,1,0:T(8,128)} %all-to-all-done.3.v_ref, bf16[256,256]{1,0:T(8,128)(2,1)} %constant.65.clone.wh, bf16[256,256]{1,0:T(8,128)(2,1)} %constant.66.clone.wl), custom_call_target="tpu_custom_call" | custom-call | flops 1610612736 | bytes 33554432 | tf_op jit(solution)/shard_map/pallas_call | solution.py:587
  206.6 42.3 %all-to-all-done.2.v_ref = f32[4,4,2,256,128]{4,3,2,1,0:T(8,128)} async-done(((f32[4,4,2,256,128]{4,3,2,1,0:T(8,128)}), f32[4,4,2,256,128]{4,3,2,1,0:T(8,128)}, u32[]{:S(2)}, u32[]{:S(2)}) %all-to-all-start.2) | async-done | bytes 4194336 | tf_op jit(solution)/shard_map/all_to_all | solution.py:578
  248.8 5.9 %shard_map.239 = (f32[2,1,32,128,128]{4,3,2,1,0:T(8,128)}, f32[2,1,32,128,128]{4,3,2,1,0:T(8,128)}) custom-call(f32[4,4,2,256,128]{4,3,2,1,0:T(8,128)} %all-to-all-done.2.v_ref, bf16[256,256]{1,0:T(8,128)(2,1)} %constant.65.clone.wh, bf16[256,256]{1,0:T(8,128)(2,1)} %constant.66.clone.wl, ...), custom_call_target="tpu_custom_call", output_to_operand_aliasing={{0}: (3, {}), {1}: (4, {})} | custom-call | flops 1610612736 | bytes 33554432 | tf_op jit(solution)/shard_map/pallas_call | solution.py:587
  (7 shorter events, 0.0 us)
Async XLA Ops:
  0.6 85.0 %copy-start = (f32[32,128,128]{2,1,0:T(8,128)S(1)}, f32[32,128,128]{2,1,0:T(8,128)}, u32[]{:S(2)}) copy-start(f32[32,128,128]{2,1,0:T(8,128)} %param.25) | copy-start | bytes 6291460
  59.0 19.4 %all-to-all-start = ((f32[32,32,128]{2,1,0:T(8,128)}), f32[32,32,128]{2,1,0:T(8,128)S(1)}, u32[]{:S(2)}, u32[]{:S(2)}) async-start(f32[32,32,128]{2,1,0:T(8,128)} %bitcast.27), calls=%async_computation | async-start | bytes 1048576 | tf_op jit(solution)/shard_map/all_to_all | solution.py:487
  78.4 0.8 copy-start.1
  82.0 18.6 %all-to-all-start.1 = ((f32[32,32,128]{2,1,0:T(8,128)}), f32[32,32,128]{2,1,0:T(8,128)S(1)}, u32[]{:S(2)}, u32[]{:S(2)}) async-start(f32[32,32,128]{2,1,0:T(8,128)} %bitcast.28), calls=%async_computation.1 | async-start | bytes 1048576 | tf_op jit(solution)/shard_map/all_to_all | solution.py:497
  100.6 0.8 copy-start.2
  142.6 53.0 %all-to-all-start.3 = ((f32[4,4,2,256,128]{4,3,2,1,0:T(8,128)}), f32[4,4,2,256,128]{4,3,2,1,0:T(8,128)}, u32[]{:S(2)}, u32[]{:S(2)}) async-start(f32[4,4,2,256,128]{4,3,2,1,0:T(8,128)} %shard_map.237), calls=%async_computation.3 | async-start | bytes 8388608 | tf_op jit(solution)/shard_map/all_to_all | solution.py:578
  195.7 53.1 %all-to-all-start.2 = ((f32[4,4,2,256,128]{4,3,2,1,0:T(8,128)}), f32[4,4,2,256,128]{4,3,2,1,0:T(8,128)}, u32[]{:S(2)}, u32[]{:S(2)}) async-start(f32[4,4,2,256,128]{4,3,2,1,0:T(8,128)} %shard_map.235), calls=%async_computation.2 | async-start | bytes 8388608 | tf_op jit(solution)/shard_map/all_to_all | solution.py:578
